TPU v7x, 32 devices: a whole 2x2x4 slice. The times are simulated.
32 devices in a mesh: row: 8 (over y, x, core), col: 4 (over z).
Axes of the slice: x: 2, y: 2, z: 4, core: 2. Of those that a mesh axis runs over, the one named last changes fastest.
Arguments:
- gradient: float32 [2048, 4608], P('row', 'col'), may hold values from -12 to 12
- first_moment: float32 [2048, 4608], P('row', 'col'), may hold values from -12 to 12, as said below
- second_moment: float32 [2048, 4608], P('row', 'col'), may hold values from 0.01 to 1
- weights: float32 [2048, 4608], P('row', 'col'), may hold values from -6 to 6
- eigenbasis: float32 [4608, 4608], P('row', 'col'), may hold values from -1 to 1, as said below
Outputs:
- new_weights: float32 [2048, 4608], P('row', 'col')
- new_first: float32 [2048, 4608], P('row', 'col')
- new_second: float32 [2048, 4608], P('row', 'col')
Inputs may be any that keep to these rules, and one draw needn't show every extreme that they name: `first_moment`: every entry's magnitude is at most 12. eigenbasis is orthogonal: its columns are orthonormal.
All inputs are finite; a program needn't handle non-finite values.
Results may differ from a plain program's by a relative error of at most 0.000059.
Values sent between devices are 32-bit elements; how exact they have to be, the bound alone decides.
No kernel may reach another device: no remote copies, remote signals or barrier semaphores. Data moves between devices by JAX's collectives and lax.ppermute only.
A program may use at most 64 MiB of HBM per device.

v0:
```python
import jax
import jax.numpy as jnp
from jax import lax
from jax.sharding import PartitionSpec as P

D = 4608
bias_first = 1.0 - 0.9**10
bias_second = 1.0 - 0.999**10
epsilon = 1e-08
step_rate = 0.25


def per_device(gradient, first_moment, second_moment, weights, eigenbasis):
    highest = lax.Precision.HIGHEST
    slab = lax.all_gather(eigenbasis, "row", axis=0, tiled=True)
    rotated = jnp.dot(
        lax.all_gather(gradient, "col", axis=1, tiled=True),
        slab,
        precision=highest,
        preferred_element_type=jnp.float32,
    )
    new_first = 0.9 * first_moment + 0.1 * rotated
    new_second = 0.999 * second_moment + 0.001 * rotated * rotated
    direction = new_first / bias_first / (jnp.sqrt(new_second / bias_second) + epsilon)
    sum_squares = lax.psum(jnp.sum(direction * direction, axis=1), "col")
    update = lax.psum_scatter(
        lax.dot_general(
            slab,
            direction,
            (((1,), (1,)), ((), ())),
            precision=highest,
            preferred_element_type=jnp.float32,
        ),
        "col",
        scatter_dimension=0,
        tiled=True,
    ).T
    row_rms = jnp.sqrt(sum_squares / D)[:, None]
    new_weights = weights - step_rate * update / jnp.maximum(1.0, row_rms)
    return (new_weights, new_first, new_second)


def solution(mesh):
    placed = (P("row", "col"), P("row", "col"), P("row", "col"), P("row", "col"), P("row", "col"))
    return jax.shard_map(
        per_device,
        mesh=mesh,
        in_specs=placed,
        out_specs=(P("row", "col"), P("row", "col"), P("row", "col")),
        check_vma=False,
    )
```

profile of v0, /device:TPU:0, one launch (start us, length us, event | category | flops | bytes accessed | tf_op | source)
XLA Modules:
  0.0 354.3 jit_solution(7112353394276214522)
XLA Ops:
  7.2 0.0 all-gather.3.cloned.1.call-start
  7.2 0.7 all-gather.3.cloned.1.call-update
  7.9 0.0 copy-start.3
  7.9 0.0 all-gather.5.cloned.1.call-start
  8.0 0.7 all-gather.5.cloned.1.call-update
  8.7 0.0 reduce-scatter.2.cloned.1.call-start
  8.7 93.0 %all-gather.3.cloned.1.call-done = f32[256,4608]{1,0:T(8,128)} async-done(((f32[256,1152]{1,0:T(8,128)}), f32[256,4608]{1,0:T(8,128)}) %all-gather.3.cloned.1.call-update) | async-done | bytes 4718608 | tf_op jit(solution)/shard_map/all_gather | solution.py:17
  101.7 108.9 %all-gather.5.cloned.1.call-done = f32[4608,1152]{1,0:T(8,128)} async-done(((f32[576,1152]{1,0:T(8,128)}), f32[4608,1152]{1,0:T(8,128)}) %all-gather.5.cloned.1.call-update) | async-done | bytes 21233680 | tf_op jit(solution)/shard_map/all_gather | solution.py:15
  210.6 0.0 copy-done.3
  210.6 0.0 copy-start
  210.6 26.6 %multiply_reduce_fusion = (f32[256]{0:T(256)S(1)}, f32[256,1152]{1,0:T(8,128)S(1)}, f32[256,1152]{1,0:T(8,128)S(1)}) fusion(f32[256,1152]{1,0:T(8,128)S(1)} %copy-done.3, f32[256,1152]{1,0:T(8,128)} %param.7, f32[256,4608]{1,0:T(8,128)} %all-gather.3.cloned.1.call-done, f32[4608,1152]{1,0:T(8,128)} %all-gather.5.cloned.1.call-done), kind=kOutput, calls=%fused_computation.4 | convolution fusion | flops 16311287808 | bytes 30671872 | tf_op jit(solution)/shard_map/dot_general | solution.py:16
  237.2 0.0 copy-start.1
  237.3 0.0 copy-start.2
  237.3 0.0 copy-done
  237.3 22.5 %convolution_bitcast_fusion = f32[4608,256]{0,1:T(8,128)} fusion(f32[4608,1152]{1,0:T(8,128)S(1)} %copy-done, f32[256,1152]{1,0:T(8,128)S(1)} %get-tuple-element.5, f32[256,1152]{1,0:T(8,128)S(1)} %get-tuple-element.4), kind=kOutput, calls=%fused_computation | convolution fusion | flops 16308633600 | bytes 28311552 | tf_op jit(solution)/shard_map/dot_general | solution.py:27
  259.8 0.0 copy-done.1
  259.8 0.0 copy-done.2
  259.8 0.0 copy-start.4
  259.8 0.0 reduce-scatter.2.cloned.1.call-update
  259.8 12.1 %psum.7 = f32[256]{0:T(256)S(1)} all-reduce(f32[256]{0:T(256)S(1)} %get-tuple-element.3), channel_id=1, replica_groups=mesh['row'=8,'col'=4] {'col'}, use_global_device_ids=true, to_apply=%region_2.0 | all-reduce | flops 256 | bytes 2048 | tf_op jit(solution)/shard_map/psum | solution.py:25
  271.9 73.4 %reduce-scatter.2.cloned.1.call-done = f32[1152,256]{0,1:T(8,128)} async-done(((f32[4608,256]{0,1:T(8,128)}), f32[1152,256]{0,1:T(8,128)}) %reduce-scatter.2.cloned.1.call-update) | async-done | bytes 1179664 | tf_op jit(solution)/shard_map/reduce_scatter | solution.py:26
  345.3 0.0 copy-done.4
  345.3 2.5 bitcast_subtract_fusion
  (1 shorter events, 0.0 us)
Async XLA Ops:
  7.2 94.5 %all-gather.3.cloned.1.call-start = ((), (), s32[]{:S(2)}) async-start(), calls=%async_computation.1 | async-start | bytes 5898240 | tf_op jit(solution)/shard_map/all_gather | solution.py:17
  7.9 202.7 %copy-start.3 = (f32[256,1152]{1,0:T(8,128)S(1)}, f32[256,1152]{1,0:T(8,128)}, u32[]{:S(2)}) copy-start(f32[256,1152]{1,0:T(8,128)} %param.6) | copy-start | bytes 3538948
  7.9 202.7 %all-gather.5.cloned.1.call-start = ((), (), s32[]{:S(2)}) async-start(), calls=%async_computation.2 | async-start | bytes 23887872 | tf_op jit(solution)/shard_map/all_gather | solution.py:15
  8.7 336.7 %reduce-scatter.2.cloned.1.call-start = ((), (), s32[]{:S(2)}) async-start(), calls=%async_computation.3 | async-start | bytes 5898240 | tf_op jit(solution)/shard_map/reduce_scatter | solution.py:26
  210.6 26.7 %copy-start = (f32[4608,1152]{1,0:T(8,128)S(1)}, f32[4608,1152]{1,0:T(8,128)}, u32[]{:S(2)}) copy-start(f32[4608,1152]{1,0:T(8,128)} %all-gather.5.cloned.1.call-done) | copy-start | bytes 63700996
  237.2 22.5 %copy-start.1 = (f32[256,1152]{1,0:T(8,128)}, f32[256,1152]{1,0:T(8,128)S(1)}, u32[]{:S(2)}) copy-start(f32[256,1152]{1,0:T(8,128)S(1)} %get-tuple-element.4) | copy-start | bytes 3538948
  237.3 22.5 %copy-start.2 = (f32[256,1152]{1,0:T(8,128)}, f32[256,1152]{1,0:T(8,128)S(1)}, u32[]{:S(2)}) copy-start(f32[256,1152]{1,0:T(8,128)S(1)} %get-tuple-element.5) | copy-start | bytes 3538948
  259.8 85.5 %copy-start.4 = (f32[256,1152]{1,0:T(8,128)S(1)}, f32[256,1152]{1,0:T(8,128)}, u32[]{:S(2)}) copy-start(f32[256,1152]{1,0:T(8,128)} %param.8) | copy-start | bytes 3538948
Sparse Core Ops, SparseCore 0:
  9.5 92.0 all-gather.2
  103.6 106.9 all-gather.4
  259.9 85.3 reduce-scatter.1
where the time goes:
time: 355 us; the launch traced here: 354 us
  waiting for transfers between devices  277 us (78%)
  matrix products  49.1 us (14%)
  between operations  13.8 us (4%)
  blocking collectives  12.1 us (3%)
    all_gather x1, waiting for transfers between devices, per_device(): slab = lax.all_gather(eigenbasis, 'row', axis=0, tiled=True)  109 us
    all_gather x1, waiting for transfers between devices, per_device(): lax.all_gather(gradient, 'col', axis=1, tiled=True)  93 us
    reduce_scatter x1, waiting for transfers between devices, per_device(): lax.psum_scatter(lax.dot_general(slab, direction, (((1,), (1,)), ((), ())...  73.4 us
    dot_general x1, matrix products, per_device(): jnp.dot(lax.all_gather(gradient, 'col', axis=1, tiled=True), slab, precis...  26.6 us
    dot_general x1, matrix products, per_device(): lax.dot_general(slab, direction, (((1,), (1,)), ((), ())), precision=high...  22.5 us
    psum x1, blocking collectives, per_device(): sum_squares = lax.psum(jnp.sum(direction * direction, axis=1), 'col')  12.1 us
  transfers between devices with their start and end apart: 3, of which 3 were waited for; matrix products, arithmetic and copies ran while one was open for 0% of the time, Pallas kernels for 0%

commit v1 on v0

--- a/solution.py
+++ b/solution.py
@@ -10,11 +10,21 @@
 step_rate = 0.25
 
 
+def gather_around(x, axis, dim):
+    ways, here, turn = (lax.axis_size(axis), lax.axis_index(axis), x.shape[dim])
+    shape = [n * ways if d == dim else n for d, n in enumerate(x.shape)]
+    full = lax.dynamic_update_slice_in_dim(jnp.zeros(shape, x.dtype), x, here * turn, axis=dim)
+    for far in range(1, ways):
+        x = lax.ppermute(x, axis, [(d, (d + 1) % ways) for d in range(ways)])
+        full = lax.dynamic_update_slice_in_dim(full, x, (here - far) % ways * turn, axis=dim)
+    return full
+
+
 def per_device(gradient, first_moment, second_moment, weights, eigenbasis):
     highest = lax.Precision.HIGHEST
     slab = lax.all_gather(eigenbasis, "row", axis=0, tiled=True)
     rotated = jnp.dot(
-        lax.all_gather(gradient, "col", axis=1, tiled=True),
+        gather_around(gradient, "col", 1),
         slab,
         precision=highest,
         preferred_element_type=jnp.float32,

time: 355 us -> 266 us (0.75)
  waiting for transfers between devices: 277 us -> 174 us
  local copies, waits for them, and re-layouts: 0.03 us -> 10.3 us
    all_gather x1 -> x0, waiting for transfers between devices: 93 us -> none  [per_device(): lax.all_gather(gradient, 'col', axis=1, tiled=True)]
    all_gather x1, waiting for transfers between devices: 109 us -> 21.9 us  [per_device(): slab = lax.all_gather(eigenbasis, 'row', axis=0, tiled=True)]
    ppermute x0 -> x3, waiting for transfers between devices: none -> 78.1 us  [gather_around(): x = lax.ppermute(x, axis, [(d, (d + 1) % ways) for d in range(ways)])]
    dynamic_update_slice x0 -> x4, local copies, waits for them, and re-layouts: none -> 7.05 us  [the longest x3 5.93 us: gather_around(): lax.dynamic_update_slice_in_dim(full, x, (here - far) % ways * turn, axis...]
  transfers between devices with their start and end apart: 3 -> 5, of which waited for: 3 -> 5; matrix products, arithmetic and copies ran while one was open for 0% -> 4% of each run, Pallas kernels for 0% -> 0%
where the time goes in v1:
time: 266 us; the launch traced here: 265 us
  waiting for transfers between devices  174 us (65%)
  matrix products  49.1 us (18%)
  between operations  14.1 us (5%)
  blocking collectives  12.1 us (5%)
  local copies, waits for them, and re-layouts  10.3 us (4%)
  starting transfers between devices  3.13 us (1%)
    ppermute x3, waiting for transfers between devices, gather_around(): x = lax.ppermute(x, axis, [(d, (d + 1) % ways) for d in range(ways)])  78.1 us
    reduce_scatter x1, waiting for transfers between devices, per_device(): lax.psum_scatter(lax.dot_general(slab, direction, (((1,), (1,)), ((), ())...  73.5 us
    dot_general x1, matrix products, per_device(): jnp.dot(gather_around(gradient, 'col', 1), slab, precision=highest, prefe...  26.7 us
    dot_general x1, matrix products, per_device(): lax.dot_general(slab, direction, (((1,), (1,)), ((), ())), precision=high...  22.4 us
    all_gather x1, waiting for transfers between devices, per_device(): slab = lax.all_gather(eigenbasis, 'row', axis=0, tiled=True)  21.9 us
    psum x1, blocking collectives, per_device(): sum_squares = lax.psum(jnp.sum(direction * direction, axis=1), 'col')  12.1 us
    dynamic_update_slice x3, local copies, waits for them, and re-layouts, gather_around(): lax.dynamic_update_slice_in_dim(full, x, (here - far) % ways * turn, axis...  5.93 us
  transfers between devices with their start and end apart: 5, of which 5 were waited for; matrix products, arithmetic and copies ran while one was open for 4% of the time, Pallas kernels for 0%

profile of v1, /device:TPU:0, one launch (start us, length us, event | category | flops | bytes accessed | tf_op | source)
XLA Modules:
  0.0 265.3 jit_solution(10869952306759583699)
XLA Ops:
  7.2 0.0 copy-start.4
  7.2 0.0 all-gather.2.cloned.1.call-start
  7.2 0.7 all-gather.2.cloned.1.call-update
  7.9 0.0 reduce-scatter.2.cloned.1.call-start
  8.0 0.5 copy-done.4
  8.4 3.1 %collective-permute-start = (f32[256,1152]{1,0:T(8,128)S(1)}, f32[256,1152]{1,0:T(8,128)S(1)}, u32[]{:S(2)}, u32[]{:S(2)}) collective-permute-start(f32[256,1152]{1,0:T(8,128)S(1)} %copy-done.4), channel_id=1, source_target_pairs={{0,1},{1,2},{2,3},{3,0},{4,5},{5,6},{6,7},{7,4},{8,9},{9,10},{10,1... | collective-permute-start | bytes 3538952 | tf_op jit(solution)/shard_map/ppermute | solution.py:18
  11.5 28.0 %collective-permute-done = f32[256,1152]{1,0:T(8,128)S(1)} collective-permute-done((f32[256,1152]{1,0:T(8,128)S(1)}, f32[256,1152]{1,0:T(8,128)S(1)}, u32[]{:S(2)}, u32[]{:S(2)}) %collective-permute-start) | collective-permute-done | bytes 1179680 | tf_op jit(solution)/shard_map/ppermute | solution.py:18
  39.5 0.0 collective-permute-start.1
  39.5 29.0 %collective-permute-done.1 = f32[256,1152]{1,0:T(8,128)} collective-permute-done((f32[256,1152]{1,0:T(8,128)S(1)}, f32[256,1152]{1,0:T(8,128)}, u32[]{:S(2)}, u32[]{:S(2)}) %collective-permute-start.1) | collective-permute-done | bytes 1179680 | tf_op jit(solution)/shard_map/ppermute | solution.py:18
  68.5 0.0 collective-permute-start.2
  68.5 2.7 %broadcast_in_dim.4 = f32[256,4608]{1,0:T(8,128)} broadcast(f32[]{:T(128)} %constant.46.clone.1), dimensions={} | broadcast | bytes 4718596 | tf_op jit(solution)/shard_map/broadcast_in_dim | solution.py:16
  71.2 1.1 constant_dynamic-update-slice_fusion.3
  72.4 1.1 constant_dynamic-update-slice_fusion.2
  73.5 2.4 constant_dynamic-update-slice_fusion.1
  75.9 0.0 copy-start.3
  75.9 21.0 %collective-permute-done.2 = f32[256,1152]{1,0:T(8,128)} collective-permute-done((f32[256,1152]{1,0:T(8,128)}, f32[256,1152]{1,0:T(8,128)}, u32[]{:S(2)}, u32[]{:S(2)}) %collective-permute-start.2) | collective-permute-done | bytes 1179680 | tf_op jit(solution)/shard_map/ppermute | solution.py:18
  96.9 2.4 constant_dynamic-update-slice_fusion
  99.3 21.9 %all-gather.2.cloned.1.call-done = f32[4608,1152]{1,0:T(8,128)} async-done(((f32[576,1152]{1,0:T(8,128)}), f32[4608,1152]{1,0:T(8,128)}) %all-gather.2.cloned.1.call-update) | async-done | bytes 21233680 | tf_op jit(solution)/shard_map/all_gather | solution.py:25
  121.2 0.0 copy-done.3
  121.2 0.0 copy-start
  121.2 26.7 %multiply_reduce_fusion = (f32[256]{0:T(256)S(1)}, f32[256,1152]{1,0:T(8,128)S(1)}, f32[256,1152]{1,0:T(8,128)S(1)}) fusion(f32[256,1152]{1,0:T(8,128)S(1)} %copy-done.3, f32[256,1152]{1,0:T(8,128)} %param.7, f32[256,4608]{1,0:T(8,128)} %constant_dynamic-update-slice_fusion, f32[4608,1152]{1,0:T(8,128)} %all-gather.2.cloned.1.call-done), kind=kOutput, calls=%fused_computation.4 | convolution fusion | flops 16311287808 | bytes 30671872 | tf_op jit(solution)/shard_map/dot_general | solution.py:26
  147.9 0.0 copy-start.1
  147.9 0.0 copy-start.2
  148.0 0.0 copy-done
  148.0 22.4 %convolution_bitcast_fusion = f32[4608,256]{0,1:T(8,128)} fusion(f32[4608,1152]{1,0:T(8,128)S(1)} %copy-done, f32[256,1152]{1,0:T(8,128)S(1)} %get-tuple-element.5, f32[256,1152]{1,0:T(8,128)S(1)} %get-tuple-element.4), kind=kOutput, calls=%fused_computation | convolution fusion | flops 16308633600 | bytes 28311552 | tf_op jit(solution)/shard_map/dot_general | solution.py:37
  170.4 0.0 copy-done.1
  170.4 0.0 copy-done.2
  170.4 0.0 copy-start.5
  170.4 0.0 reduce-scatter.2.cloned.1.call-update
  170.4 12.1 %psum.7 = f32[256]{0:T(256)S(1)} all-reduce(f32[256]{0:T(256)S(1)} %get-tuple-element.3), channel_id=1, replica_groups=mesh['row'=8,'col'=4] {'col'}, use_global_device_ids=true, to_apply=%region_2.3 | all-reduce | flops 256 | bytes 2048 | tf_op jit(solution)/shard_map/psum | solution.py:35
  182.5 73.5 %reduce-scatter.2.cloned.1.call-done = f32[1152,256]{0,1:T(8,128)} async-done(((f32[4608,256]{0,1:T(8,128)}), f32[1152,256]{0,1:T(8,128)}) %reduce-scatter.2.cloned.1.call-update) | async-done | bytes 1179664 | tf_op jit(solution)/shard_map/reduce_scatter | solution.py:36
  256.0 0.0 copy-done.5
  256.0 2.5 bitcast_subtract_fusion
  (1 shorter events, 0.0 us)
Async XLA Ops:
  7.2 1.3 copy-start.4
  7.2 114.0 %all-gather.2.cloned.1.call-start = ((), (), s32[]{:S(2)}) async-start(), calls=%async_computation.1 | async-start | bytes 23887872 | tf_op jit(solution)/shard_map/all_gather | solution.py:25
  7.9 248.0 %reduce-scatter.2.cloned.1.call-start = ((), (), s32[]{:S(2)}) async-start(), calls=%async_computation.2 | async-start | bytes 5898240 | tf_op jit(solution)/shard_map/reduce_scatter | solution.py:36
  8.4 31.0 %collective-permute-start = (f32[256,1152]{1,0:T(8,128)S(1)}, f32[256,1152]{1,0:T(8,128)S(1)}, u32[]{:S(2)}, u32[]{:S(2)}) collective-permute-start(f32[256,1152]{1,0:T(8,128)S(1)} %copy-done.4), channel_id=1, source_target_pairs={{0,1},{1,2},{2,3},{3,0},{4,5},{5,6},{6,7},{7,4},{8,9},{9,10},{10,1... | collective-permute-start | bytes 3538952 | tf_op jit(solution)/shard_map/ppermute | solution.py:18
  39.5 29.0 %collective-permute-start.1 = (f32[256,1152]{1,0:T(8,128)S(1)}, f32[256,1152]{1,0:T(8,128)}, u32[]{:S(2)}, u32[]{:S(2)}) collective-permute-start(f32[256,1152]{1,0:T(8,128)S(1)} %collective-permute-done), channel_id=1, source_target_pairs={{0,1},{1,2},{2,3},{3,0},{4,5},{5,6},{6,7},{7,4},{8,9},{9,10},{10,1... | collective-permute-start | bytes 3538952 | tf_op jit(solution)/shard_map/ppermute | solution.py:18
  68.5 28.4 %collective-permute-start.2 = (f32[256,1152]{1,0:T(8,128)}, f32[256,1152]{1,0:T(8,128)}, u32[]{:S(2)}, u32[]{:S(2)}) collective-permute-start(f32[256,1152]{1,0:T(8,128)} %collective-permute-done.1), channel_id=1, source_target_pairs={{0,1},{1,2},{2,3},{3,0},{4,5},{5,6},{6,7},{7,4},{8,9},{9,10},{10,1... | collective-permute-start | bytes 3538952 | tf_op jit(solution)/shard_map/ppermute | solution.py:18
  75.9 45.3 %copy-start.3 = (f32[256,1152]{1,0:T(8,128)S(1)}, f32[256,1152]{1,0:T(8,128)}, u32[]{:S(2)}) copy-start(f32[256,1152]{1,0:T(8,128)} %param.6) | copy-start | bytes 3538948
  121.2 26.8 %copy-start = (f32[4608,1152]{1,0:T(8,128)S(1)}, f32[4608,1152]{1,0:T(8,128)}, u32[]{:S(2)}) copy-start(f32[4608,1152]{1,0:T(8,128)} %all-gather.2.cloned.1.call-done) | copy-start | bytes 63700996
  147.9 22.5 %copy-start.1 = (f32[256,1152]{1,0:T(8,128)}, f32[256,1152]{1,0:T(8,128)S(1)}, u32[]{:S(2)}) copy-start(f32[256,1152]{1,0:T(8,128)S(1)} %get-tuple-element.4) | copy-start | bytes 3538948
  147.9 22.4 %copy-start.2 = (f32[256,1152]{1,0:T(8,128)}, f32[256,1152]{1,0:T(8,128)S(1)}, u32[]{:S(2)}) copy-start(f32[256,1152]{1,0:T(8,128)S(1)} %get-tuple-element.5) | copy-start | bytes 3538948
  170.4 85.6 %copy-start.5 = (f32[256,1152]{1,0:T(8,128)S(1)}, f32[256,1152]{1,0:T(8,128)}, u32[]{:S(2)}) copy-start(f32[256,1152]{1,0:T(8,128)} %param.8) | copy-start | bytes 3538948
Sparse Core Ops, SparseCore 0:
  9.9 111.2 all-gather.1
  170.5 85.3 reduce-scatter.1
